TPU v7x, 32 devices: a whole 2x2x4 slice. The times are simulated.
32 devices in a mesh: dp: 8 (over z, x), mp: 4 (over y, core).
Axes of the slice: x: 2, y: 2, z: 4, core: 2. Of those that a mesh axis runs over, the one named last changes fastest.
Arguments:
- hidden: bfloat16 [8, 512, 4608], P('dp', 'mp'), may hold values from -6 to 6
- lengths: int32 [8], P('dp'), may hold values from 64 to 512
- norm_gain: float32 [4608], replicated, may hold values from 0.25 to 1.75
- w_query: bfloat16 [4608, 2048], P('dp', 'mp'), may hold values from -0.09375 to 0.09375
- w_key: bfloat16 [4608, 1024], P('dp', 'mp'), may hold values from -0.09375 to 0.09375
- w_value: bfloat16 [4608, 1024], P('dp', 'mp'), may hold values from -0.09375 to 0.09375
- w_out: bfloat16 [2048, 4608], P('mp', 'dp'), may hold values from -0.125 to 0.125
- post_gain: float32 [4608], replicated, may hold values from 0.25 to 1.75
Outputs:
- mixed: bfloat16 [8, 512, 4608], P('dp', 'mp')
- key_cache: bfloat16 [8, 512, 1024], P('dp', None, 'mp')
- value_cache: bfloat16 [8, 512, 1024], P('dp', None, 'mp')
All inputs are finite; a program needn't handle non-finite values.
Results may differ from a plain program's by a relative error of at most 0.01.
Values may be sent and summed in bfloat16 or wider, within the bound.
A program may use at most 128 MiB of HBM per device.

v0:
```python
import jax
import jax.numpy as jnp
from jax import lax
from jax.sharding import PartitionSpec as P

HD = 128


def rotate(values, positions):
    half = values.shape[-1] // 2
    freqs = 10000.0 ** (-jnp.arange(half, dtype=jnp.float32) / half)
    angles = positions.astype(jnp.float32)[:, None] * freqs[None, :]
    cosine = jnp.cos(angles)[:, None, :]
    sine = jnp.sin(angles)[:, None, :]
    first = values[..., :half]
    second = values[..., half:]
    return jnp.concatenate(
        [first * cosine - second * sine, second * cosine + first * sine], axis=-1
    )


def attend(query_rows, key_rows, value_rows, row_index, length):
    score = jnp.einsum("qkgd,tkd->kgqt", query_rows, key_rows, preferred_element_type=jnp.float32)
    score = 50.0 * jnp.tanh(score / 50.0)
    key_index = jnp.arange(key_rows.shape[0], dtype=jnp.int32)
    keep = (key_index[None, :] <= row_index[:, None]) & (key_index[None, :] < length)
    score = jnp.where(keep[None, None], score, -1e30)
    top = jnp.max(score, axis=-1, keepdims=True)
    expo = jnp.exp(score - top)
    weights = (expo / jnp.sum(expo, axis=-1, keepdims=True)).astype(jnp.bfloat16)
    return jnp.einsum(
        "kgqt,tkd->qkgd", weights, value_rows, preferred_element_type=jnp.float32
    ).astype(jnp.bfloat16)


def local(hidden, lengths, norm_gain, w_query, w_key, w_value, w_out, post_gain):
    rollouts, local_len, width = hidden.shape
    maxlen = local_len * lax.axis_size("mp")
    q_heads = w_query.shape[1] // HD
    kv_heads = w_key.shape[1] // HD
    group = q_heads // kv_heads
    rows_f = hidden.astype(jnp.float32)
    normed = (
        rows_f * lax.rsqrt(jnp.mean(rows_f * rows_f, axis=-1, keepdims=True) + 1e-06) * norm_gain
    ).astype(jnp.bfloat16)
    gathered = lax.all_gather(normed, "mp", axis=1, tiled=True)
    flat = gathered.reshape(rollouts * maxlen, width)
    pieces = (
        lax.all_gather(w_query, "dp", axis=0, tiled=True),
        lax.all_gather(w_key, "dp", axis=0, tiled=True),
        lax.all_gather(w_value, "dp", axis=0, tiled=True),
    )
    qraw, kraw, vraw = tuple(
        (jnp.dot(flat, piece, preferred_element_type=jnp.float32) for piece in pieces)
    )
    positions = jnp.arange(maxlen, dtype=jnp.int32)
    query = (
        rotate(qraw.reshape(rollouts, maxlen, q_heads, HD), positions) * 144.0 ** (-0.5)
    ).astype(jnp.bfloat16)
    key = rotate(kraw.reshape(rollouts, maxlen, kv_heads, HD), positions).astype(jnp.bfloat16)
    value = vraw.reshape(rollouts, maxlen, kv_heads, HD).astype(jnp.bfloat16)
    grouped = query.reshape(rollouts, maxlen, kv_heads, group, HD)
    length = lengths[0]
    outputs = [attend(grouped[0], key[0], value[0], positions, length)]
    attended = jnp.stack(outputs).reshape(rollouts * maxlen, q_heads * HD)
    partial_value = (
        jnp.dot(
            attended,
            lax.all_gather(w_out, "dp", axis=1, tiled=True),
            preferred_element_type=jnp.float32,
        )
        .astype(jnp.bfloat16)
        .astype(jnp.float32)
    )
    projected = lax.psum_scatter(
        partial_value.reshape(rollouts, maxlen, width).astype(jnp.bfloat16),
        "mp",
        scatter_dimension=1,
        tiled=True,
    ).astype(jnp.float32)
    post = (
        projected
        * lax.rsqrt(jnp.mean(projected * projected, axis=-1, keepdims=True) + 1e-06)
        * post_gain
    )
    own_rows = lax.axis_index("mp") * local_len + jnp.arange(local_len, dtype=jnp.int32)
    live_local = (own_rows[None, :] < lengths[:, None])[:, :, None]
    mixed = jnp.where(live_local, rows_f + post, 0.0).astype(jnp.bfloat16)
    live_all = (positions[None, :] < lengths[:, None])[:, :, None]
    key_cache = jnp.where(
        live_all, key.reshape(rollouts, maxlen, kv_heads * HD), jnp.zeros((), jnp.bfloat16)
    )
    value_cache = jnp.where(
        live_all, value.reshape(rollouts, maxlen, kv_heads * HD), jnp.zeros((), jnp.bfloat16)
    )
    return (mixed, key_cache, value_cache)


def solution(mesh):
    return jax.shard_map(
        local,
        mesh=mesh,
        in_specs=(
            P("dp", "mp", None),
            P("dp"),
            P(),
            P("dp", "mp"),
            P("dp", "mp"),
            P("dp", "mp"),
            P("mp", "dp"),
            P(),
        ),
        out_specs=(P("dp", "mp", None), P("dp", None, "mp"), P("dp", None, "mp")),
        check_vma=False,
    )
```

profile of v0, /device:TPU:0, one launch (start us, length us, event | category | flops | bytes accessed | tf_op | source)
XLA Modules:
  0.0 381.2 jit_solution(8354099245536206741)
XLA Ops:
  7.2 0.0 all-gather.10.cloned.1.call-start
  7.2 0.7 all-gather.10.cloned.1.call-update
  7.9 0.0 all-gather.8.cloned.1.call-start
  7.9 0.7 all-gather.8.cloned.1.call-update
  8.6 0.0 all-gather.6.cloned.1.call-start
  8.7 1.6 fusion.11
  10.3 2.6 fusion.13
  12.9 0.0 all-gather.6.cloned.1.call-update
  12.9 0.0 all-gather.12.cloned.1.call-start
  13.0 0.5 all-gather.12.cloned.1.call-update
  13.5 0.0 all-gather.14.cloned.1.call-start
  13.6 0.5 all-gather.14.cloned.1.call-update
  14.1 0.0 reduce-scatter.2.cloned.1.call-start
  14.8 0.8 fusion.32
  15.7 0.5 multiply_cosine_fusion
  16.2 48.5 %all-gather.10.cloned.1.call-done = bf16[4608,256]{1,0:T(8,128)(2,1)} async-done(((bf16[576,256]{1,0:T(8,128)(2,1)}), bf16[4608,256]{1,0:T(8,128)(2,1)}) %all-gather.10.cloned.1.call-update) | async-done | bytes 2359312 | tf_op jit(solution)/shard_map/all_gather | solution.py:50
  64.7 4.3 %copy.12 = bf16[256,4608]{1,0:T(8,128)(2,1)} copy(bf16[256,4608]{0,1:T(8,128)(2,1)} %bitcast.78) | data formatting | bytes 4718592 | tf_op jit(solution)/shard_map/dot_general | solution.py:54
  69.0 48.2 %all-gather.8.cloned.1.call-done = bf16[4608,256]{1,0:T(8,128)(2,1)} async-done(((bf16[576,256]{1,0:T(8,128)(2,1)}), bf16[4608,256]{1,0:T(8,128)(2,1)}) %all-gather.8.cloned.1.call-update) | async-done | bytes 2359312 | tf_op jit(solution)/shard_map/all_gather | solution.py:51
  117.3 2.8 copy.11
  120.1 35.3 %all-gather.6.cloned.1.call-done = bf16[1,512,4608]{2,1,0:T(8,128)(2,1)} async-done(((bf16[1,128,4608]{2,1,0:T(8,128)(2,1)}), bf16[1,512,4608]{2,1,0:T(8,128)(2,1)}) %all-gather.6.cloned.1.call-update) | async-done | bytes 4718608 | tf_op jit(solution)/shard_map/all_gather | solution.py:46
  155.4 0.0 copy-start.3
  155.4 4.6 %fusion.25 = f32[1,512,2,128]{1,3,2,0:T(8,128)S(1)} fusion(bf16[2,128,4608]{2,1,0:T(8,128)(2,1)} %bitcast.81, bf16[1,512,4608]{2,1,0:T(8,128)(2,1)} %all-gather.6.cloned.1.call-done), kind=kOutput, calls=%fused_computation.32 | convolution fusion | flops 1207959552 | bytes 7602176 | tf_op jit(solution)/shard_map/dot_general | solution.py:54
  160.1 0.1 subtract_convert_fusion
  160.2 0.0 copy-done.3
  160.2 1.4 fusion.28
  161.6 75.2 %all-gather.12.cloned.1.call-done = bf16[4608,512]{1,0:T(8,128)(2,1)} async-done(((bf16[576,512]{1,0:T(8,128)(2,1)}), bf16[4608,512]{1,0:T(8,128)(2,1)}) %all-gather.12.cloned.1.call-update) | async-done | bytes 4718608 | tf_op jit(solution)/shard_map/all_gather | solution.py:49
  236.8 6.7 %copy.13 = bf16[512,4608]{1,0:T(8,128)(2,1)} copy(bf16[512,4608]{0,1:T(8,128)(2,1)} %bitcast.76) | data formatting | bytes 9437184 | tf_op jit(solution)/shard_map/dot_general | solution.py:54
  243.5 6.4 %fusion.21 = f32[1,512,4,128]{1,3,2,0:T(8,128)S(1)} fusion(bf16[4,128,4608]{2,1,0:T(8,128)(2,1)} %bitcast.77, bf16[1,512,4608]{2,1,0:T(8,128)(2,1)} %all-gather.6.cloned.1.call-done), kind=kOutput, calls=%fused_computation.30 | convolution fusion | flops 2415919104 | bytes 10485760 | tf_op jit(solution)/shard_map/dot_general | solution.py:54
  249.9 0.2 multiply_subtract_fusion
  250.1 0.0 copy-start.1
  250.1 0.3 copy.15
  250.4 0.3 copy.14
  250.8 0.3 fusion.31
  251.1 0.0 copy-done.1
  251.2 1.9 fusion.53
  253.1 2.4 fusion.24
  255.5 61.1 %all-gather.14.cloned.1.call-done = bf16[512,4608]{0,1:T(8,128)(2,1)} async-done(((bf16[512,576]{0,1:T(8,128)(2,1)}), bf16[512,4608]{0,1:T(8,128)(2,1)}) %all-gather.14.cloned.1.call-update) | async-done | bytes 4718608 | tf_op jit(solution)/shard_map/all_gather | solution.py:69
  316.6 6.7 %fusion.1 = bf16[1,512,4608]{2,1,0:T(8,128)(2,1)} fusion(bf16[512,512]{0,1:T(8,128)(2,1)S(1)} %bitcast.90, bf16[512,4608]{0,1:T(8,128)(2,1)} %all-gather.14.cloned.1.call-done), kind=kOutput, calls=%fused_computation.2 | convolution fusion | flops 2418278400 | bytes 9961472 | tf_op jit(solution)/shard_map/dot_general | solution.py:67
  323.3 0.0 copy-start
  323.3 0.0 copy-start.2
  323.3 0.0 reduce-scatter.2.cloned.1.call-update
  323.4 0.1 copy.19
  323.5 0.1 copy.18
  323.7 0.9 broadcast_select_fusion
  324.6 45.2 %reduce-scatter.2.cloned.1.call-done = bf16[1,128,4608]{2,1,0:T(8,128)(2,1)} async-done(((bf16[1,512,4608]{2,1,0:T(8,128)(2,1)}), bf16[1,128,4608]{2,1,0:T(8,128)(2,1)}) %reduce-scatter.2.cloned.1.call-update) | async-done | bytes 1179664 | tf_op jit(solution)/shard_map/reduce_scatter | solution.py:75
  369.8 1.6 fusion.9
  371.4 0.0 copy-done
  371.4 0.0 copy-done.2
  371.4 2.9 fusion.15
  (7 shorter events, 0.1 us)
Async XLA Ops:
  7.2 57.6 %all-gather.10.cloned.1.call-start = ((), (), s32[]{:S(2)}) async-start(), calls=%async_computation.3 | async-start | bytes 2654208 | tf_op jit(solution)/shard_map/all_gather | solution.py:50
  7.9 109.4 %all-gather.8.cloned.1.call-start = ((), (), s32[]{:S(2)}) async-start(), calls=%async_computation.2 | async-start | bytes 2654208 | tf_op jit(solution)/shard_map/all_gather | solution.py:51
  8.6 146.8 %all-gather.6.cloned.1.call-start = ((), (), s32[]{:S(2)}) async-start(), calls=%async_computation.1 | async-start | bytes 5898240 | tf_op jit(solution)/shard_map/all_gather | solution.py:46
  12.9 223.9 %all-gather.12.cloned.1.call-start = ((), (), s32[]{:S(2)}) async-start(), calls=%async_computation.4 | async-start | bytes 5308416 | tf_op jit(solution)/shard_map/all_gather | solution.py:49
  13.5 303.1 %all-gather.14.cloned.1.call-start = ((), (), s32[]{:S(2)}) async-start(), calls=%async_computation.5 | async-start | bytes 5308416 | tf_op jit(solution)/shard_map/all_gather | solution.py:69
  14.1 355.7 %reduce-scatter.2.cloned.1.call-start = ((), (), s32[]{:S(2)}) async-start(), calls=%async_computation.6 | async-start | bytes 5898240 | tf_op jit(solution)/shard_map/reduce_scatter | solution.py:75
  155.4 4.7 %copy-start.3 = (bf16[1,512,4608]{2,1,0:T(8,128)(2,1)S(1)}, bf16[1,512,4608]{2,1,0:T(8,128)(2,1)}, u32[]{:S(2)}) copy-start(bf16[1,512,4608]{2,1,0:T(8,128)(2,1)} %all-gather.6.cloned.1.call-done) | copy-start | bytes 14155780
  250.1 1.0 copy-start.1
  323.3 48.1 %copy-start = (bf16[1,128,4608]{2,1,0:T(8,128)(2,1)S(1)}, bf16[1,128,4608]{2,1,0:T(8,128)(2,1)}, u32[]{:S(2)}) copy-start(bf16[1,128,4608]{2,1,0:T(8,128)(2,1)} %param.8) | copy-start | bytes 3538948
  323.3 48.1 %copy-start.2 = (f32[4608]{0:T(1024)S(1)}, f32[4608]{0:T(1024)}, u32[]{:S(2)}) copy-start(f32[4608]{0:T(1024)} %param.15) | copy-start | bytes 55300
Sparse Core Ops, SparseCore 0:
  10.2 54.5 all-gather.9
  66.9 50.3 all-gather.7
  119.4 35.9 all-gather.5
  157.5 79.3 all-gather.11
  238.9 77.6 all-gather.13
  323.5 46.3 reduce-scatter.1
where the time goes:
time: 382 us; the launch traced here: 381 us
  waiting for transfers between devices  316 us (83%)
  matrix products  23.5 us (6%)
  between operations  14.9 us (4%)
  local copies, waits for them, and re-layouts  14.8 us (4%)
  other arithmetic  11.6 us (3%)
    all_gather x1, waiting for transfers between devices, local(): lax.all_gather(w_query, 'dp', axis=0, tiled=True)  75.2 us
    all_gather x1, waiting for transfers between devices, local(): lax.all_gather(w_out, 'dp', axis=1, tiled=True)  61.1 us
    all_gather x1, waiting for transfers between devices, local(): lax.all_gather(w_key, 'dp', axis=0, tiled=True)  48.5 us
    all_gather x1, waiting for transfers between devices, local(): lax.all_gather(w_value, 'dp', axis=0, tiled=True)  48.2 us
    reduce_scatter x1, waiting for transfers between devices, local(): lax.psum_scatter(partial_value.reshape(rollouts, maxlen, width).astype(jn...  45.2 us
    all_gather x1, waiting for transfers between devices, local(): gathered = lax.all_gather(normed, 'mp', axis=1, tiled=True)  35.3 us
    dot_general x3, local copies, waits for them, and re-layouts, local(): jnp.dot(flat, piece, preferred_element_type=jnp.float32)  13.9 us
    dot_general x3, matrix products, local(): jnp.dot(flat, piece, preferred_element_type=jnp.float32)  12.4 us
  transfers between devices with their start and end apart: 6, of which 6 were waited for; matrix products, arithmetic and copies ran while one was open for 10% of the time, Pallas kernels for 0%

commit v1 on v0

--- a/solution.py
+++ b/solution.py
@@ -4,6 +4,21 @@
 from jax.sharding import PartitionSpec as P
 
 HD = 128
+
+
+def launch_ladders(local_array, dimension_no):
+    shard_axis = "mp"
+    axis_total = lax.psum(1, axis_name=shard_axis)
+    known = sorted(((kk, (kk + 1) % axis_total) for kk in range(axis_total)))
+    local_out = local_array
+    ledger = [local_out]
+    for tick in tuple(range(1, axis_total)):
+        local_out = lax.ppermute(local_out, axis_name=shard_axis, perm=known)
+        ledger.insert(0, local_out)
+    tall = jnp.concatenate(ledger, axis=dimension_no)
+    y_new = lax.axis_index(shard_axis) + 1
+    x_next = jnp.roll(tall, y_new * local_array.shape[dimension_no], axis=dimension_no)
+    return x_next
 
 
 def rotate(values, positions):
@@ -43,7 +58,7 @@
     normed = (
         rows_f * lax.rsqrt(jnp.mean(rows_f * rows_f, axis=-1, keepdims=True) + 1e-06) * norm_gain
     ).astype(jnp.bfloat16)
-    gathered = lax.all_gather(normed, "mp", axis=1, tiled=True)
+    gathered = launch_ladders(normed, 1)
     flat = gathered.reshape(rollouts * maxlen, width)
     pieces = (
         lax.all_gather(w_query, "dp", axis=0, tiled=True),

time: 382 us -> 342 us (0.90)
  waiting for transfers between devices: 316 us -> 255 us
  local copies, waits for them, and re-layouts: 14.8 us -> 25.1 us
  matrix products: 23.5 us -> 29 us
  other arithmetic: 11.6 us -> 16.5 us
    all_gather x1, waiting for transfers between devices: 48.5 us -> 0.01 us  [local(): lax.all_gather(w_key, 'dp', axis=0, tiled=True)]
    ppermute x0 -> x3, waiting for transfers between devices: none -> 44.3 us  [launch_ladders(): local_out = lax.ppermute(local_out, axis_name=shard_axis, perm=known)]
    all_gather x1 -> x0, waiting for transfers between devices: 35.3 us -> none  [local(): gathered = lax.all_gather(normed, 'mp', axis=1, tiled=True)]
    unnamed x8 -> x28, local copies, waits for them, and re-layouts: 0.02 us -> 9.26 us
    all_gather x1, waiting for transfers between devices: 75.2 us -> 67.1 us  [local(): lax.all_gather(w_query, 'dp', axis=0, tiled=True)]
    all_gather x1, waiting for transfers between devices: 48.2 us -> 40.3 us  [local(): lax.all_gather(w_value, 'dp', axis=0, tiled=True)]
    all_gather x1, waiting for transfers between devices: 61.1 us -> 56.1 us  [local(): lax.all_gather(w_out, 'dp', axis=1, tiled=True)]
  transfers between devices with their start and end apart: 6 -> 8, of which waited for: 6 -> 7; matrix products, arithmetic and copies ran while one was open for 10% -> 17% of each run, Pallas kernels for 0% -> 0%
where the time goes in v1:
time: 342 us; the launch traced here: 341 us
  waiting for transfers between devices  255 us (75%)
  matrix products  29 us (8%)
  local copies, waits for them, and re-layouts  25.1 us (7%)
  other arithmetic  16.5 us (5%)
  between operations  14.7 us (4%)
    all_gather x1, waiting for transfers between devices, local(): lax.all_gather(w_query, 'dp', axis=0, tiled=True)  67.1 us
    all_gather x1, waiting for transfers between devices, local(): lax.all_gather(w_out, 'dp', axis=1, tiled=True)  56.1 us
    reduce_scatter x1, waiting for transfers between devices, local(): lax.psum_scatter(partial_value.reshape(rollouts, maxlen, width).astype(jn...  45.2 us
    ppermute x3, waiting for transfers between devices, launch_ladders(): local_out = lax.ppermute(local_out, axis_name=shard_axis, perm=known)  44.3 us
    all_gather x1, waiting for transfers between devices, local(): lax.all_gather(w_value, 'dp', axis=0, tiled=True)  40.3 us
    dot_general x3, matrix products, local(): jnp.dot(flat, piece, preferred_element_type=jnp.float32)  15.8 us
    dot_general x3, local copies, waits for them, and re-layouts, local(): jnp.dot(flat, piece, preferred_element_type=jnp.float32)  13.8 us
    unnamed x28, local copies, waits for them, and re-layouts  9.26 us
  transfers between devices with their start and end apart: 8, of which 7 were waited for; matrix products, arithmetic and copies ran while one was open for 17% of the time, Pallas kernels for 0%

profile of v1, /device:TPU:0, one launch (start us, length us, event | category | flops | bytes accessed | tf_op | source)
XLA Modules:
  0.0 341.2 jit_solution(10807734696642469752)
XLA Ops:
  7.2 0.0 all-gather.7.cloned.1.call-start
  7.2 0.7 all-gather.7.cloned.1.call-update
  7.9 0.0 all-gather.5.cloned.1.call-start
  7.9 0.7 all-gather.5.cloned.1.call-update
  8.6 0.0 all-gather.9.cloned.1.call-start
  8.7 0.7 all-gather.9.cloned.1.call-update
  9.4 0.0 all-gather.11.cloned.1.call-start
  9.4 1.6 fusion.14
  11.0 1.6 fusion.16
  12.6 0.0 copy-start
  12.7 0.5 collective-permute-start
  13.2 15.8 %collective-permute-done = bf16[1,128,4608]{2,1,0:T(8,128)(2,1)S(1)} collective-permute-done((bf16[1,128,4608]{2,1,0:T(8,128)(2,1)S(1)}, bf16[1,128,4608]{2,1,0:T(8,128)(2,1)S(1)}, u32[]{:S(2)}, u32[]{:S(2)}) %collective-permute-start) | collective-permute-done | bytes 1179680 | tf_op jit(solution)/shard_map/ppermute | solution.py:16
  29.0 0.0 collective-permute-start.1
  29.0 15.6 %collective-permute-done.1 = bf16[1,128,4608]{2,1,0:T(8,128)(2,1)S(1)} collective-permute-done((bf16[1,128,4608]{2,1,0:T(8,128)(2,1)S(1)}, bf16[1,128,4608]{2,1,0:T(8,128)(2,1)S(1)}, u32[]{:S(2)}, u32[]{:S(2)}) %collective-permute-start.1) | collective-permute-done | bytes 1179680 | tf_op jit(solution)/shard_map/ppermute | solution.py:16
  44.7 0.0 collective-permute-start.2
  44.7 0.0 all-gather.11.cloned.1.call-update
  44.7 0.0 reduce-scatter.2.cloned.1.call-start
  45.4 0.0 copy-start.9
  45.5 0.8 fusion.35
  46.3 1.2 multiply_cosine_fusion
  47.5 12.9 %collective-permute-done.2 = bf16[1,128,4608]{2,1,0:T(8,128)(2,1)} collective-permute-done((bf16[1,128,4608]{2,1,0:T(8,128)(2,1)S(1)}, bf16[1,128,4608]{2,1,0:T(8,128)(2,1)}, u32[]{:S(2)}, u32[]{:S(2)}) %collective-permute-start.2) | collective-permute-done | bytes 1179680 | tf_op jit(solution)/shard_map/ppermute | solution.py:16
  60.4 2.4 constant_dynamic-update-slice_fusion.7
  62.8 1.1 constant_dynamic-update-slice_fusion.6
  63.9 1.1 constant_dynamic-update-slice_fusion.5
  65.0 0.0 copy-done
  65.0 0.0 copy-done.9
  65.0 1.4 constant_dynamic-update-slice_fusion.4
  66.3 2.4 constant_dynamic-update-slice_fusion.3
  68.7 1.1 constant_dynamic-update-slice_fusion.2
  69.9 1.1 constant_dynamic-update-slice_fusion.1
  71.0 1.4 constant_dynamic-update-slice_fusion
  72.4 4.3 %copy.12 = bf16[256,4608]{1,0:T(8,128)(2,1)} copy(bf16[256,4608]{0,1:T(8,128)(2,1)} %bitcast.78) | data formatting | bytes 4718592 | tf_op jit(solution)/shard_map/dot_general | solution.py:69
  76.8 40.3 %all-gather.5.cloned.1.call-done = bf16[4608,256]{1,0:T(8,128)(2,1)} async-done(((bf16[576,256]{1,0:T(8,128)(2,1)}), bf16[4608,256]{1,0:T(8,128)(2,1)}) %all-gather.5.cloned.1.call-update) | async-done | bytes 2359312 | tf_op jit(solution)/shard_map/all_gather | solution.py:66
  117.1 2.8 copy.11
  119.9 0.0 copy-start.1
  120.0 0.0 copy-start.3
  120.0 4.5 %fusion.28 = f32[1,512,2,128]{1,3,2,0:T(8,128)S(1)} fusion(bf16[2,128,4608]{2,1,0:T(8,128)(2,1)} %bitcast.81, bf16[1,1024,4608]{2,1,0:T(8,128)(2,1)} %constant_dynamic-update-slice_fusion, s32[]{:T(128)S(6)} %select_n.45), kind=kOutput, calls=%fused_computation.35 | convolution fusion | flops 1207959552 | bytes 7602180 | tf_op jit(solution)/shard_map/dot_general | solution.py:69
  124.5 0.0 copy-done.1
  124.5 0.0 copy-done.3
  124.5 0.8 subtract_convert_fusion
  125.3 4.8 %fusion.31 = bf16[512,2,128]{0,2,1:T(8,128)(2,1)} fusion(bf16[2,128,4608]{2,1,0:T(8,128)(2,1)S(1)} %bitcast.80, bf16[1,1024,4608]{2,1,0:T(8,128)(2,1)} %constant_dynamic-update-slice_fusion, s32[]{:T(128)S(6)} %select_n.45), kind=kOutput, calls=%fused_computation.36 | convolution fusion | flops 1208090624 | bytes 7340036 | tf_op jit(solution)/shard_map/dot_general | solution.py:69
  130.1 67.1 %all-gather.9.cloned.1.call-done = bf16[4608,512]{1,0:T(8,128)(2,1)} async-done(((bf16[576,512]{1,0:T(8,128)(2,1)}), bf16[4608,512]{1,0:T(8,128)(2,1)}) %all-gather.9.cloned.1.call-update) | async-done | bytes 4718608 | tf_op jit(solution)/shard_map/all_gather | solution.py:64
  197.2 6.7 %copy.13 = bf16[512,4608]{1,0:T(8,128)(2,1)} copy(bf16[512,4608]{0,1:T(8,128)(2,1)} %bitcast.76) | data formatting | bytes 9437184 | tf_op jit(solution)/shard_map/dot_general | solution.py:69
  203.9 6.5 %fusion.24 = f32[1,512,4,128]{1,3,2,0:T(8,128)S(1)} fusion(bf16[4,128,4608]{2,1,0:T(8,128)(2,1)} %bitcast.77, bf16[1,1024,4608]{2,1,0:T(8,128)(2,1)} %constant_dynamic-update-slice_fusion, s32[]{:T(128)S(6)} %select_n.45), kind=kOutput, calls=%fused_computation.33 | convolution fusion | flops 2415919104 | bytes 10485764 | tf_op jit(solution)/shard_map/dot_general | solution.py:69
  210.4 0.0 copy-done.2
  210.4 0.0 copy-done.4
  210.4 0.0 copy-start.6
  210.5 0.0 copy-start.7
  210.5 1.0 multiply_subtract_fusion
  211.5 0.3 copy.14
  211.8 1.4 copy.15
  213.2 1.1 fusion.34
  214.3 0.0 copy-done.6
  214.3 3.1 fusion.59
  217.5 3.4 fusion.27
  220.9 56.1 %all-gather.11.cloned.1.call-done = bf16[512,4608]{0,1:T(8,128)(2,1)} async-done(((bf16[512,576]{0,1:T(8,128)(2,1)}), bf16[512,4608]{0,1:T(8,128)(2,1)}) %all-gather.11.cloned.1.call-update) | async-done | bytes 4718608 | tf_op jit(solution)/shard_map/all_gather | solution.py:84
  277.0 6.7 %fusion.1 = bf16[1,512,4608]{2,1,0:T(8,128)(2,1)} fusion(bf16[512,512]{0,1:T(8,128)(2,1)S(1)} %bitcast.90, bf16[512,4608]{0,1:T(8,128)(2,1)} %all-gather.11.cloned.1.call-done), kind=kOutput, calls=%fused_computation.2 | convolution fusion | flops 2418278400 | bytes 9961472 | tf_op jit(solution)/shard_map/dot_general | solution.py:82
  283.7 0.0 reduce-scatter.2.cloned.1.call-update
  283.7 0.1 copy.18
  283.9 0.1 copy.19
  284.0 0.9 broadcast_select_fusion
  284.9 45.2 %reduce-scatter.2.cloned.1.call-done = bf16[1,128,4608]{2,1,0:T(8,128)(2,1)} async-done(((bf16[1,512,4608]{2,1,0:T(8,128)(2,1)}), bf16[1,128,4608]{2,1,0:T(8,128)(2,1)}) %reduce-scatter.2.cloned.1.call-update) | async-done | bytes 1179664 | tf_op jit(solution)/shard_map/reduce_scatter | solution.py:90
  330.2 1.6 fusion.12
  331.8 2.9 fusion.18
  (17 shorter events, 0.1 us)
Async XLA Ops:
  7.2 65.3 %all-gather.7.cloned.1.call-start = ((), (), s32[]{:S(2)}) async-start(), calls=%async_computation.2 | async-start | bytes 2654208 | tf_op jit(solution)/shard_map/all_gather | solution.py:65
  7.9 109.2 %all-gather.5.cloned.1.call-start = ((), (), s32[]{:S(2)}) async-start(), calls=%async_computation.1 | async-start | bytes 2654208 | tf_op jit(solution)/shard_map/all_gather | solution.py:66
  8.6 188.6 %all-gather.9.cloned.1.call-start = ((), (), s32[]{:S(2)}) async-start(), calls=%async_computation.3 | async-start | bytes 5308416 | tf_op jit(solution)/shard_map/all_gather | solution.py:64
  9.4 267.6 %all-gather.11.cloned.1.call-start = ((), (), s32[]{:S(2)}) async-start(), calls=%async_computation.4 | async-start | bytes 5308416 | tf_op jit(solution)/shard_map/all_gather | solution.py:84
  12.6 52.3 %copy-start = (bf16[1,128,4608]{2,1,0:T(8,128)(2,1)S(1)}, bf16[1,128,4608]{2,1,0:T(8,128)(2,1)}, u32[]{:S(2)}) copy-start(bf16[1,128,4608]{2,1,0:T(8,128)(2,1)} %param.8) | copy-start | bytes 3538948
  12.7 16.4 %collective-permute-start = (bf16[1,128,4608]{2,1,0:T(8,128)(2,1)S(1)}, bf16[1,128,4608]{2,1,0:T(8,128)(2,1)S(1)}, u32[]{:S(2)}, u32[]{:S(2)}) collective-permute-start(bf16[1,128,4608]{2,1,0:T(8,128)(2,1)S(1)} %fusion.16), channel_id=1, source_target_pairs={{0,1},{1,2},{2,3},{3,0},{4,5},{5,6},{6,7},{7,4},{8,9},{9,10},{10,1... | collective-permute-start | bytes 3538952 | tf_op jit(solution)/shard_map/ppermute | solution.py:16
  29.0 15.6 %collective-permute-start.1 = (bf16[1,128,4608]{2,1,0:T(8,128)(2,1)S(1)}, bf16[1,128,4608]{2,1,0:T(8,128)(2,1)S(1)}, u32[]{:S(2)}, u32[]{:S(2)}) collective-permute-start(bf16[1,128,4608]{2,1,0:T(8,128)(2,1)S(1)} %collective-permute-done), channel_id=1, source_target_pairs={{0,1},{1,2},{2,3},{3,0},{4,5},{5,6},{6,7},{7,4},{8,9},{9,10},{10,1... | collective-permute-start | bytes 3538952 | tf_op jit(solution)/shard_map/ppermute | solution.py:16
  44.7 15.7 %collective-permute-start.2 = (bf16[1,128,4608]{2,1,0:T(8,128)(2,1)S(1)}, bf16[1,128,4608]{2,1,0:T(8,128)(2,1)}, u32[]{:S(2)}, u32[]{:S(2)}) collective-permute-start(bf16[1,128,4608]{2,1,0:T(8,128)(2,1)S(1)} %collective-permute-done.1), channel_id=1, source_target_pairs={{0,1},{1,2},{2,3},{3,0},{4,5},{5,6},{6,7},{7,4},{8,9},{9,10},{10,1... | collective-permute-start | bytes 3538952 | tf_op jit(solution)/shard_map/ppermute | solution.py:16
  44.7 285.5 %reduce-scatter.2.cloned.1.call-start = ((), (), s32[]{:S(2)}) async-start(), calls=%async_computation.5 | async-start | bytes 5898240 | tf_op jit(solution)/shard_map/reduce_scatter | solution.py:90
  45.4 19.6 %copy-start.9 = (f32[4608]{0:T(1024)S(1)}, f32[4608]{0:T(1024)}, u32[]{:S(2)}) copy-start(f32[4608]{0:T(1024)} %param.10) | copy-start | bytes 55300
  119.9 4.6 %copy-start.1 = (f32[512,64]{0,1:T(8,128)S(1)}, f32[512,64]{0,1:T(8,128)}, u32[]{:S(2)}) copy-start(f32[512,64]{0,1:T(8,128)} %get-tuple-element.7) | copy-start | bytes 393220
  120.0 4.6 %copy-start.3 = (f32[512,64]{0,1:T(8,128)S(1)}, f32[512,64]{0,1:T(8,128)}, u32[]{:S(2)}) copy-start(f32[512,64]{0,1:T(8,128)} %get-tuple-element.8) | copy-start | bytes 393220
  203.9 6.5 %copy-start.2 = (f32[512,64]{0,1:T(8,128)S(1)}, f32[512,64]{0,1:T(8,128)}, u32[]{:S(2)}) copy-start(f32[512,64]{0,1:T(8,128)} %get-tuple-element.7) | copy-start | bytes 393220
  203.9 6.5 %copy-start.4 = (f32[512,64]{0,1:T(8,128)S(1)}, f32[512,64]{0,1:T(8,128)}, u32[]{:S(2)}) copy-start(f32[512,64]{0,1:T(8,128)} %get-tuple-element.8) | copy-start | bytes 393220
  210.4 3.9 %copy-start.6 = (bf16[1,512,2,64]{1,3,2,0:T(8,128)(2,1)S(1)}, bf16[1,512,2,64]{1,3,2,0:T(8,128)(2,1)}, u32[]{:S(2)}) copy-start(bf16[1,512,2,64]{1,3,2,0:T(8,128)(2,1)} %get-tuple-element.5) | copy-start | bytes 393220
  210.5 3.9 %copy-start.7 = (bf16[1,512,2,64]{1,3,2,0:T(8,128)(2,1)S(1)}, bf16[1,512,2,64]{1,3,2,0:T(8,128)(2,1)}, u32[]{:S(2)}) copy-start(bf16[1,512,2,64]{1,3,2,0:T(8,128)(2,1)} %get-tuple-element.6) | copy-start | bytes 393220
  214.3 3.1 copy-start.5
  214.3 3.1 copy-start.8
  283.7 48.1 %copy-start.10 = (f32[4608]{0:T(1024)S(1)}, f32[4608]{0:T(1024)}, u32[]{:S(2)}) copy-start(f32[4608]{0:T(1024)} %param.15) | copy-start | bytes 55300
Sparse Core Ops, SparseCore 0:
  10.2 54.3 all-gather.6
  66.7 50.3 all-gather.4
  119.3 77.8 all-gather.8
  199.3 77.6 all-gather.10
  283.8 46.3 reduce-scatter.1
